TPU v7x, 32 devices: a whole 2x2x4 slice. The times are simulated.
32 devices in a mesh: grp: 2 (over y), band: 4 (over z), mem: 2 (over x), fld: 2 (over core).
Axes of the slice: x: 2, y: 2, z: 4, core: 2. Of those that a mesh axis runs over, the one named last changes fastest.
Arguments:
- surface_fields: bfloat16 [16, 8, 8, 65536], P(('grp', 'mem'), 'fld', None, 'band'), parts along dimension 0, may hold values from -8 to 8
- land_mask: int32 [65536], P('band'), may hold values from 0 to 1, as said below
- source_area: float32 [65536], P('band'), may hold values from 0.5 to 1.5
- target_area: float32 [16384], P('band'), may hold values from 0.75 to 1.25
- weight_tiles: bfloat16 [16, 128, 128], replicated, may hold values from -1 to 1
- tile_of: int32 [128, 24], P('band'), may hold values from 0 to 15
- block_of: int32 [128, 24], P('band'), may hold values from 0 to 191, as said below
- live_slots: int32 [128], P('band'), may hold values from 1 to 24, as said below
Outputs:
- regridded: float32 [16, 8, 8, 16384], P(('grp', 'mem'), 'fld', None, 'band'), parts along dimension 0
- conserved: float32 [16, 8, 8], P(('grp', 'mem'), 'fld'), parts along dimension 0
- ensemble: float32 [16, 8], P(('grp', 'fld')), parts along dimension 0
There are 2 independent parts, one for each index of `grp`. A program takes and returns all parts, laid end to end along the dimension named above; an argument that names none is the same for every part. Nothing has to cross between parts.
Inputs may be any that keep to these rules, and one draw needn't show every extreme that they name: `land_mask`: 1 marks ocean, 0 land. `block_of`: for the target block at place j (0 to 31) within its band, every entry lies in 4 * j to 4 * j + 4 + 2 * 32 - 1; values under 32 name the lower band's last blocks, values from 160 on the higher band's first blocks. `live_slots`: slots from this count on are unused.
All inputs are finite; a program needn't handle non-finite values.
Results may differ from a plain program's by a relative error of at most 0.0014.
Values may be sent and summed in bfloat16 or wider, within the bound.
A program may use at most 64 MiB of HBM per device.

v0:
```python
import functools

import jax
import jax.numpy as jnp
from jax import lax
from jax.experimental import pallas as pl
from jax.experimental.pallas import tpu as pltpu
from jax.sharding import PartitionSpec as P

HALO_BLK = 32
SEND_TYPE = jnp.float32
MESH = pl.DeviceIdType.MESH
HBM = pl.BlockSpec(memory_space=pltpu.HBM)
VMEM = pl.BlockSpec(memory_space=pltpu.VMEM)


def row_of(sums):
    return jnp.sum(sums.T, axis=0, keepdims=True)


def slot_dot(source, held, table, n, slots, shift, low, high):
    tiles, blocks, live = table
    used, zero_tile = live(n), held.shape[0] - 1
    left, right = [], []
    for k in range(slots):
        block = blocks(k, n) - shift
        keep = (k < used) & (block >= low) & (block < high)
        left.append(source[jnp.where(keep, block, low)])
        right.append(held[jnp.where(keep, tiles(k, n), zero_tile)])
    return jnp.dot(
        jnp.concatenate(left, axis=1),
        jnp.concatenate(right, axis=0),
        preferred_element_type=jnp.float32,
    )


def main_kernel(
    bands, mems, edge,
    fields, mask_h, area_h, target_area_h, tiles, tile_h, block_h, live_h,
    raw, totals, fix_ref,
    mask, area, target_area, tile_s, block_s, live_s,
    stage, source, held, made, came, rows, landed, target_sum,
    tile_in, block_in, live_in, tile_n, block_n, live_n,
    load_sem, small_sem, list_sem, table_send, table_recv, edge_send, edge_recv, row_send, row_recv,
):
    band, mem = lax.axis_index("band"), lax.axis_index("mem")
    count = bands * mems
    me = mem * bands + band
    own, columns, tile = source.shape
    slots, targets = tile_h.shape
    has_low, has_high = band > 0, band < bands - 1
    chunk = HALO_BLK * tile
    chunks = own // HALO_BLK
    order = [0, chunks - 1] + list(range(1, chunks - 1))

    def place(step):
        other = lax.rem(me + step, count)
        return {"mem": other // bands, "band": lax.rem(other, bands)}

    barrier = pltpu.get_barrier_semaphore()

    def greet(step, carry):
        pl.semaphore_signal(barrier, inc=1, device_id=place(step), device_id_type=MESH)
        return carry

    lax.fori_loop(1, count, greet, 0)

    loads = [
        pltpu.make_async_copy(
            fields.at[:, :, pl.ds(c * chunk, chunk)],
            stage.at[:, :, pl.ds(c * chunk, chunk)],
            load_sem.at[c],
        )
        for c in range(chunks)
    ]
    small = [
        pltpu.make_async_copy(a, b, small_sem.at[i])
        for i, (a, b) in enumerate((
            (mask_h, mask),
            (area_h, area),
            (tiles, held.at[pl.ds(0, tiles.shape[0])]),
            (tile_h, tile_s),
            (block_h, block_s),
            (live_h, live_s),
            (target_area_h, target_area),
        ))
    ]
    small[0].start()
    small[1].start()
    for c in order[:2]:
        loads[c].start()
    for copy in small[2:]:
        copy.start()
    for c in order[2:]:
        loads[c].start()

    pl.semaphore_wait(barrier, count - 1)

    def table_copies(way):
        to = {"band": band - 1 if way == 0 else band + 1}
        pairs = ((tile_h, tile_in), (block_h, block_in), (live_h, live_in))
        return [
            pltpu.make_async_remote_copy(
                src_ref=mine,
                dst_ref=theirs.at[way],
                send_sem=table_send.at[way, i],
                recv_sem=table_recv.at[way, i],
                device_id=to,
                device_id_type=MESH,
            )
            for i, (mine, theirs) in enumerate(pairs)
        ]

    def edge_copy(way, j):
        return pltpu.make_async_remote_copy(
            src_ref=made.at[way, j],
            dst_ref=came.at[way, j],
            send_sem=edge_send.at[way, j],
            recv_sem=edge_recv.at[way, j],
            device_id={"band": band + 1 if way == 0 else band - 1},
            device_id_type=MESH,
        )

    for way, there in ((0, has_low), (1, has_high)):
        @pl.when(there)
        def _(way=way):
            for copy in table_copies(way):
                copy.start()

    held[tiles.shape[0]] = jnp.zeros((tile, tile), held.dtype)

    def fetch(pairs):
        copies = [
            pltpu.make_async_copy(a, b, list_sem.at[i]) for i, (a, b) in enumerate(pairs)
        ]
        for copy in copies:
            copy.start()
        for copy in copies:
            copy.wait()

    def weigh(c, running):
        loads[c].wait()

        def one(n, running):
            at = pl.ds(pl.multiple_of(n * tile, tile), tile)
            scale = area[:, at] * mask[:, at].astype(jnp.float32)
            part = stage[:, :, at].astype(jnp.float32).reshape(columns, tile) * scale
            part = part.astype(source.dtype)
            source[n] = part
            return running + part.astype(jnp.float32)

        return lax.fori_loop(c * HALO_BLK, (c + 1) * HALO_BLK, one, running, unroll=4)

    source_sum = jnp.zeros((columns, tile), jnp.float32)
    small[0].wait()
    small[1].wait()
    for c in order:
        source_sum = weigh(c, source_sum)

    own_table = (
        lambda k, n: tile_s[k, n],
        lambda k, n: block_s[k, n],
        lambda n: live_s[0, n],
    )

    def own_group(first, width, carry):
        for u in range(width):
            t = first + u
            at = pl.ds(pl.multiple_of(t * tile, tile), tile)
            value = slot_dot(source, held, own_table, t, slots, HALO_BLK, 0, own)
            raw[t] = value * (1.0 / target_area[:, at])
            carry = carry + value
        return carry

    for copy in small[2:]:
        copy.wait()
    target_sum[...] = own_group(0, edge // 2, jnp.zeros((columns, tile), jnp.float32))

    for way, there in ((0, has_high), (1, has_low)):
        @pl.when(there)
        def _(way=way):
            for copy in table_copies(way):
                copy.wait_recv()
            pairs = ((tile_in, tile_n), (block_in, block_n), (live_in, live_n))
            fetch([(a.at[way], b.at[way]) for a, b in pairs])

        @pl.when(jnp.logical_not(there))
        def _(way=way):
            pairs = ((tile_h, tile_n), (block_h, block_n), (live_h, live_n))
            fetch([(a, b.at[way]) for a, b in pairs])

    reaches = (
        (HALO_BLK - own, own - HALO_BLK, own),
        (HALO_BLK + own, 0, HALO_BLK),
    )

    def one_edge(j, carry):
        for way, there in ((0, has_high), (1, has_low)):
            table = (
                lambda k, n, way=way: tile_n[way, k, n],
                lambda k, n, way=way: block_n[way, k, n],
                lambda n, way=way: live_n[way, 0, n],
            )
            first = 0 if way == 0 else targets - edge
            value = slot_dot(source, held, table, first + j, slots, *reaches[way])
            made[way, j] = value.astype(made.dtype)
            carry = carry + value * there.astype(jnp.float32)

        for way, there in ((0, has_high), (1, has_low)):
            @pl.when((j > 0) & there)
            def _(way=way):
                edge_copy(way, j - 1).start()

        return carry

    edge_total = lax.fori_loop(0, edge, one_edge, target_sum[...])
    target_sum[...] = edge_total

    target_sum[...] = own_group(edge // 2, edge // 2, target_sum[...])
    for way, there in ((0, has_high), (1, has_low)):
        @pl.when(there)
        def _(way=way):
            edge_copy(way, edge - 1).start()

    target_total = lax.fori_loop(
        1, targets // edge, lambda g, carry: own_group(g * edge, edge, carry), target_sum[...]
    )
    rows[0:1, :] = row_of(source_sum)
    rows[1:2, :] = row_of(target_total)
    rows[2:3, :] = jnp.broadcast_to(
        jnp.sum(target_area[...], axis=1, keepdims=True), (1, columns)
    )
    rows[3:8, :] = jnp.zeros((5, columns), jnp.float32)

    def row_copy(step):
        return pltpu.make_async_remote_copy(
            src_ref=rows,
            dst_ref=landed.at[step],
            send_sem=row_send.at[step],
            recv_sem=row_recv.at[step],
            device_id=place(step),
            device_id_type=MESH,
        )

    def begin(step, carry):
        row_copy(step).start()
        return carry

    def end(step, carry):
        row_copy(step).wait()
        return carry

    for way, there in ((0, has_low), (1, has_high)):
        @pl.when(there)
        def _(way=way):
            for copy in table_copies(way):
                copy.wait_send()

    lax.fori_loop(1, count, begin, 0)
    landed[0] = rows[...]

    for way, there in ((0, has_low), (1, has_high)):
        @pl.when(there)
        def _(way=way):
            def add(j, carry):
                edge_copy(way, j).wait_recv()
                t = j if way == 0 else targets - edge + j
                at = pl.ds(pl.multiple_of(t * tile, tile), tile)
                share = 1.0 / target_area[:, at]
                raw[t] = raw[t] + came[way, j].astype(jnp.float32) * share
                return carry

            lax.fori_loop(0, edge, add, 0)

    for way, there in ((0, has_high), (1, has_low)):
        @pl.when(there)
        def _(way=way):
            def sent(j, carry):
                edge_copy(way, j).wait_send()
                return carry

            lax.fori_loop(0, edge, sent, 0)

    lax.fori_loop(1, count, end, 0)
    for m in range(mems):
        total = jnp.zeros(rows.shape, jnp.float32)
        for b in range(bands):
            total = total + landed[lax.rem(me - (m * bands + b) + count, count)]
        totals[m] = total
    mine = totals[mem]
    fix = (mine[0:1, :] - mine[1:2, :]) / mine[2:3, :]
    fix_ref[...] = jnp.broadcast_to(fix, (fix_ref.shape[1], fix.shape[1])).T


def main_call(fields, mask, area, target_area, tiles, tile_t, block_t, live):
    bands, mems = lax.axis_size("band"), lax.axis_size("mem")
    rows, snaps, cells = fields.shape
    columns = rows * snaps
    slots, targets = tile_t.shape
    count, tile = tiles.shape[0], tiles.shape[1]
    own = cells // tile
    edge = HALO_BLK // (own // targets)
    dma = pltpu.SemaphoreType.DMA
    peers = bands * mems
    return pl.pallas_call(
        functools.partial(main_kernel, bands, mems, edge),
        in_specs=[HBM] * 8,
        out_specs=(VMEM, VMEM, VMEM),
        out_shape=(
            jax.ShapeDtypeStruct((targets, columns, tile), jnp.float32),
            jax.ShapeDtypeStruct((mems, 8, columns), jnp.float32),
            jax.ShapeDtypeStruct((columns, tile), jnp.float32),
        ),
        scratch_shapes=[
            pltpu.VMEM(mask.shape, mask.dtype),
            pltpu.VMEM(area.shape, area.dtype),
            pltpu.VMEM(target_area.shape, target_area.dtype),
            pltpu.SMEM(tile_t.shape, tile_t.dtype),
            pltpu.SMEM(block_t.shape, block_t.dtype),
            pltpu.SMEM(live.shape, live.dtype),
            pltpu.VMEM(fields.shape, fields.dtype),
            pltpu.VMEM((own, columns, tile), jnp.bfloat16),
            pltpu.VMEM((count + 1, tile, tile), tiles.dtype),
            pltpu.VMEM((2, edge, columns, tile), SEND_TYPE),
            pltpu.VMEM((2, edge, columns, tile), SEND_TYPE),
            pltpu.VMEM((8, columns), jnp.float32),
            pltpu.VMEM((peers, 8, columns), jnp.float32),
            pltpu.VMEM((columns, tile), jnp.float32),
            pltpu.VMEM((2, slots, targets), jnp.int32),
            pltpu.VMEM((2, slots, targets), jnp.int32),
            pltpu.VMEM((2, 1, targets), jnp.int32),
            pltpu.SMEM((2, slots, targets), jnp.int32),
            pltpu.SMEM((2, slots, targets), jnp.int32),
            pltpu.SMEM((2, 1, targets), jnp.int32),
            dma((own // HALO_BLK,)),
            dma((7,)),
            dma((3,)),
            dma((2, 3)),
            dma((2, 3)),
            dma((2, edge)),
            dma((2, edge)),
            dma((peers,)),
            dma((peers,)),
        ],
        compiler_params=pltpu.CompilerParams(
            collective_id=0, has_side_effects=True, vmem_limit_bytes=32 << 20
        ),
    )(*[pltpu.with_memory_space_constraint(a, pltpu.HBM) for a in (fields, mask, area, target_area, tiles, tile_t, block_t, live)])


def finish_kernel(fields, snaps, raw_ref, fix_ref, totals_ref, out_ref, mean_ref, ensemble_ref):
    count, columns, tile = raw_ref.shape
    fix = fix_ref[...]
    for n in range(count):
        value = raw_ref[n] + fix
        out_ref[:, :, n * tile:(n + 1) * tile] = value.reshape(columns // snaps, snaps, tile)

    @pl.when(pl.program_id(0) == 1)
    def _():
        mems, members = totals_ref.shape[0], mean_ref.shape[0]
        spot = lax.broadcasted_iota(jnp.int32, (columns, tile), 0)
        lane = lax.broadcasted_iota(jnp.int32, (columns, tile), 1)
        chosen = lax.rem(spot, snaps) == lane
        summed = jnp.zeros((fields, snaps), jnp.float32)

        def table(m):
            row = totals_ref[m, 0:1, :] / totals_ref[m, 2:3, :]
            column = jnp.broadcast_to(row, (tile, columns)).T
            spread = jnp.where(chosen, column, 0.0).reshape(columns // snaps, snaps, tile)
            return jnp.sum(spread, axis=1)[:, 0:snaps]

        mine = table(lax.axis_index("mem"))
        for n in range(members):
            mean_ref[n] = mine[n * fields:(n + 1) * fields]
        for m in range(mems):
            all_of = table(m)
            for n in range(members):
                summed = summed + all_of[n * fields:(n + 1) * fields]
        ensemble_ref[...] = summed / (mems * members)


def finish(raw, fix, totals, members, fields, snaps):
    targets, columns, tile = raw.shape
    steps = 2
    part = targets // steps
    rows = members * fields
    return pl.pallas_call(
        functools.partial(finish_kernel, fields, snaps),
        grid=(steps,),
        in_specs=[
            pl.BlockSpec((part, columns, tile), lambda i: (i, 0, 0)),
            pl.BlockSpec((columns, tile), lambda i: (0, 0)),
            pl.BlockSpec(totals.shape, lambda i: (0, 0, 0)),
        ],
        out_specs=(
            pl.BlockSpec((rows, snaps, part * tile), lambda i: (0, 0, i)),
            pl.BlockSpec((members, fields, snaps), lambda i: (0, 0, 0)),
            pl.BlockSpec((fields, snaps), lambda i: (0, 0)),
        ),
        out_shape=(
            jax.ShapeDtypeStruct((rows, snaps, targets * tile), jnp.float32),
            jax.ShapeDtypeStruct((members, fields, snaps), jnp.float32),
            jax.ShapeDtypeStruct((fields, snaps), jnp.float32),
        ),
        compiler_params=pltpu.CompilerParams(vmem_limit_bytes=16 << 20),
    )(raw, fix, totals)


def on_device(
    surface_fields, land_mask, source_area, target_area, weight_tiles, tile_of, block_of, live_slots
):
    members, fields, snaps, cells = surface_fields.shape
    targets = tile_of.shape[0]
    target_cells = target_area.shape[0]
    raw, totals, fix = main_call(
        surface_fields.reshape(members * fields, snaps, cells),
        land_mask.reshape(1, cells),
        source_area.reshape(1, cells),
        target_area.reshape(1, target_cells),
        weight_tiles,
        tile_of.T,
        block_of.T,
        live_slots.reshape(1, targets),
    )
    regridded, conserved, ensemble = finish(raw, fix, totals, members, fields, snaps)
    return regridded.reshape(members, fields, snaps, target_cells), conserved, ensemble


def solution(mesh):
    placed = (
        P(("grp", "mem"), "fld", None, "band"),
        P("band"),
        P("band"),
        P("band"),
        P(),
        P("band", None),
        P("band", None),
        P("band"),
    )
    return jax.shard_map(
        on_device,
        mesh=mesh,
        in_specs=placed,
        out_specs=(
            P(("grp", "mem"), "fld", None, "band"),
            P(("grp", "mem"), "fld", None),
            P(("grp", "fld"), None),
        ),
        check_vma=False,
    )
```

profile of v0, /device:TPU:0, one launch (start us, length us, event | category | flops | bytes accessed | tf_op | source)
XLA Modules:
  0.0 28.6 jit_solution(15077263279095160401)
XLA Ops:
  0.6 26.5 %shard_map.103 = (f32[32,128,128]{2,1,0:T(8,128)S(1)}, f32[2,8,128]{2,1,0:T(8,128)S(1)}, f32[128,128]{1,0:T(8,128)S(1)}) custom-call(bf16[16,8,16384]{2,1,0:T(8,128)(2,1)} %bitcast.8, s32[1,16384]{1,0:T(1,128)} %bitcast.9, f32[1,16384]{1,0:T(1,128)} %bitcast.10, f32[1,4096]{1,0:T(1,128)} %bitcast.11, bf16[16,128,128]{2,1,0:T(8,128)(2,1)} %tiles.1, ...), custom_call_target="tpu_custom_call" | custom-call | tf_op jit(solution)/shard_map/pallas_call | solution.py:305
  27.1 1.5 %shard_map.104 = (f32[16,8,4096]{2,1,0:T(8,128)}, f32[4,4,8]{2,1,0:T(4,128)}, f32[4,8]{1,0:T(4,128)}) custom-call(f32[32,128,128]{2,1,0:T(8,128)S(1)} %get-tuple-element.9.raw_ref, f32[128,128]{1,0:T(8,128)S(1)} %get-tuple-element.10.fix_ref, f32[2,8,128]{2,1,0:T(8,128)S(1)} %get-tuple-element.11.totals_ref), custom_call_target="tpu_custom_call" | custom-call | tf_op jit(solution)/shard_map/pallas_call | solution.py:387
where the time goes:
time: 28.8 us; the launch traced here: 28.6 us
  Pallas kernels  28 us (97%)
  between operations  0.64 us (2%)
    pallas_call x1, Pallas kernels, main_call(): pl.pallas_call(functools.partial(main_kernel, bands, mems, edge), in_spec...  26.5 us
    pallas_call x1, Pallas kernels, finish(): pl.pallas_call(functools.partial(finish_kernel, fields, snaps), grid=(ste...  1.46 us

commit v1 on v0

--- a/solution.py
+++ b/solution.py
@@ -8,7 +8,7 @@
 from jax.sharding import PartitionSpec as P
 
 HALO_BLK = 32
-SEND_TYPE = jnp.float32
+SEND_TYPE = jnp.bfloat16
 MESH = pl.DeviceIdType.MESH
 HBM = pl.BlockSpec(memory_space=pltpu.HBM)
 VMEM = pl.BlockSpec(memory_space=pltpu.VMEM)

time: 28.8 us -> 28.4 us (0.986)
  Pallas kernels: 28 us -> 27.6 us
    pallas_call x1, Pallas kernels: 26.5 us -> 26.1 us  [main_call(): pl.pallas_call(functools.partial(main_kernel, bands, mems, edge), in_spec...]
where the time goes in v1:
time: 28.4 us; the launch traced here: 28.2 us
  Pallas kernels  27.6 us (97%)
  between operations  0.64 us (2%)
    pallas_call x1, Pallas kernels, main_call(): pl.pallas_call(functools.partial(main_kernel, bands, mems, edge), in_spec...  26.1 us
    pallas_call x1, Pallas kernels, finish(): pl.pallas_call(functools.partial(finish_kernel, fields, snaps), grid=(ste...  1.46 us

profile of v1, /device:TPU:0, one launch (start us, length us, event | category | flops | bytes accessed | tf_op | source)
XLA Modules:
  0.0 28.2 jit_solution(7399364600380698565)
XLA Ops:
  0.6 26.1 %shard_map.103 = (f32[32,128,128]{2,1,0:T(8,128)S(1)}, f32[2,8,128]{2,1,0:T(8,128)S(1)}, f32[128,128]{1,0:T(8,128)S(1)}) custom-call(bf16[16,8,16384]{2,1,0:T(8,128)(2,1)} %bitcast.8, s32[1,16384]{1,0:T(1,128)} %bitcast.9, f32[1,16384]{1,0:T(1,128)} %bitcast.10, f32[1,4096]{1,0:T(1,128)} %bitcast.11, bf16[16,128,128]{2,1,0:T(8,128)(2,1)} %tiles.1, ...), custom_call_target="tpu_custom_call" | custom-call | tf_op jit(solution)/shard_map/pallas_call | solution.py:305
  26.7 1.5 %shard_map.104 = (f32[16,8,4096]{2,1,0:T(8,128)}, f32[4,4,8]{2,1,0:T(4,128)}, f32[4,8]{1,0:T(4,128)}) custom-call(f32[32,128,128]{2,1,0:T(8,128)S(1)} %get-tuple-element.9.raw_ref, f32[128,128]{1,0:T(8,128)S(1)} %get-tuple-element.10.fix_ref, f32[2,8,128]{2,1,0:T(8,128)S(1)} %get-tuple-element.11.totals_ref), custom_call_target="tpu_custom_call" | custom-call | tf_op jit(solution)/shard_map/pallas_call | solution.py:387

commit v2 on v1

v2 whole, which is shorter than its diff:
```python
import functools

import jax
import jax.numpy as jnp
from jax import lax
from jax.experimental import pallas as pl
from jax.experimental.pallas import tpu as pltpu
from jax.sharding import PartitionSpec as P

HALO_BLK = 32
SEND_TYPE = jnp.bfloat16
MESH = pl.DeviceIdType.MESH
HBM = pl.BlockSpec(memory_space=pltpu.HBM)
VMEM = pl.BlockSpec(memory_space=pltpu.VMEM)


def row_of(sums):
    return jnp.sum(sums.T, axis=0, keepdims=True)


def slot_dot(source, held, table, n, slots, shift, low, high):
    used, zero_tile = table[2 * slots, n], held.shape[0] - 1
    left, right = [], []
    for k in range(slots):
        block = table[slots + k, n] - shift
        keep = (k < used) & (block >= low) & (block < high)
        left.append(source[jnp.where(keep, block, low)])
        right.append(held[jnp.where(keep, table[k, n], zero_tile)])
    return jnp.dot(
        jnp.concatenate(left, axis=1),
        jnp.concatenate(right, axis=0),
        preferred_element_type=jnp.float32,
    )


def slot_marks(table, slots, shift, there, own, count):
    targets = table.shape[1]
    pieces = slots // 8
    blank = jnp.full((8, 128 - pieces * targets), -1, jnp.int32)
    live = (lax.broadcasted_iota(jnp.int32, (slots, targets), 0) < table[2 * slots:2 * slots + 1]) & there
    blocks = jnp.where(live, table[slots:2 * slots] - shift, -1)
    kinds = table[0:slots]
    rows = [jnp.concatenate([a[8 * p:8 * p + 8] for p in range(pieces)] + [blank], axis=1) for a in (blocks, kinds)]
    spot = lax.broadcasted_iota(jnp.int32, (own, 128), 0)
    kind = lax.broadcasted_iota(jnp.int32, (count, 128), 0)
    left = [jnp.where(rows[0][r:r + 1] == spot, 1.0, 0.0).astype(jnp.bfloat16) for r in range(8)]
    right = [jnp.where(rows[1][r:r + 1] == kind, 1.0, 0.0).astype(jnp.bfloat16) for r in range(8)]
    return left, right


def main_kernel(
    bands, mems, edge,
    fields, mask_h, area_h, target_area_h, tiles, tile_h, block_h, live_h,
    raw, totals, fix_ref,
    mask, area, target_area, table_v, table_s, near_v, near_s,
    stage, source, held, made, came, rows, landed, source_sum, target_sum, tile_sum, coef,
    load_sem, small_sem, near_sem, table_send, table_recv, edge_send, edge_recv, row_send, row_recv, token,
):
    band, mem = lax.axis_index("band"), lax.axis_index("mem")
    count = bands * mems
    me = mem * bands + band
    own, columns, tile = source.shape
    slots, targets = tile_h.shape
    kinds = tiles.shape[0]
    has_low, has_high = band > 0, band < bands - 1
    chunk = HALO_BLK * tile
    chunks = own // HALO_BLK
    order = [0, chunks - 1] + list(range(1, chunks - 1))
    ways = ((0, has_high), (1, has_low))

    def neighbour(way):
        return {"band": band + 1 if way == 0 else band - 1}

    barrier = pltpu.get_barrier_semaphore()
    for way, there in ways:
        @pl.when(there)
        def _(way=way):
            pl.semaphore_signal(barrier, inc=1, device_id=neighbour(way), device_id_type=MESH)
    for step in range(1, mems):
        pl.semaphore_signal(
            barrier, inc=1, device_id={"mem": lax.rem(mem + step, mems)}, device_id_type=MESH
        )

    loads = [
        pltpu.make_async_copy(
            fields.at[:, :, pl.ds(c * chunk, chunk)],
            stage.at[:, :, pl.ds(c * chunk, chunk)],
            load_sem.at[c],
        )
        for c in range(chunks)
    ]
    lists = ((tile_h, pl.ds(0, slots)), (block_h, pl.ds(slots, slots)), (live_h, pl.ds(2 * slots, 1)))
    small = [
        pltpu.make_async_copy(a, b, small_sem.at[i])
        for i, (a, b) in enumerate(
            [(a, table_v.at[at]) for a, at in lists]
            + [(mask_h, mask), (area_h, area)]
            + [(a, table_s.at[at]) for a, at in lists]
            + [(tiles, held.at[pl.ds(0, kinds)]), (target_area_h, target_area)]
        )
    ]
    for copy in small[:5]:
        copy.start()
    for c in order[:2]:
        loads[c].start()
    for copy in small[5:]:
        copy.start()
    for c in order[2:]:
        loads[c].start()

    def stand_in(way):
        return [
            pltpu.make_async_copy(a, b.at[way, at], near_sem.at[way, i])
            for i, (a, b, at) in enumerate(
                [(a, near_v, at) for a, at in lists] + [(a, near_s, at) for a, at in lists]
            )
        ]

    for way, there in ways:
        @pl.when(jnp.logical_not(there))
        def _(way=way):
            for copy in stand_in(way):
                copy.start()

    def table_copies(way):
        return [
            pltpu.make_async_remote_copy(
                src_ref=table_v,
                dst_ref=theirs.at[1 - way],
                send_sem=table_send.at[way, i],
                recv_sem=table_recv.at[1 - way, i],
                device_id=neighbour(way),
                device_id_type=MESH,
            )
            for i, theirs in enumerate((near_s, near_v))
        ]

    def edge_copy(way, j):
        return pltpu.make_async_remote_copy(
            src_ref=made.at[way, j],
            dst_ref=came.at[way, j],
            send_sem=edge_send.at[way, j],
            recv_sem=edge_recv.at[way, j],
            device_id=neighbour(way),
            device_id_type=MESH,
        )

    held[kinds] = jnp.zeros((tile, tile), held.dtype)
    source_sum[...] = jnp.zeros((columns, tile), jnp.float32)
    target_sum[...] = jnp.zeros((columns, tile), jnp.float32)

    def weigh(c):
        loads[c].wait()

        def one(n, running):
            at = pl.ds(pl.multiple_of(n * tile, tile), tile)
            scale = area[:, at] * mask[:, at].astype(jnp.float32)
            part = stage[:, :, at].astype(jnp.float32).reshape(columns, tile) * scale
            part = part.astype(source.dtype)
            source[n] = part
            return running + part.astype(jnp.float32)

        source_sum[...] = lax.fori_loop(
            c * HALO_BLK, (c + 1) * HALO_BLK, one, source_sum[...], unroll=4
        )

    def token_step(up, down):
        for way, at, first in ((0, up, band == 0), (1, down, band == bands - 1)):
            there = has_high if way == 0 else has_low

            @pl.when(at & jnp.logical_not(first))
            def _(way=way):
                pl.semaphore_wait(token.at[way], 1)

            @pl.when(at & there)
            def _(way=way):
                pl.semaphore_signal(
                    token.at[way], inc=1, device_id=neighbour(way), device_id_type=MESH
                )

    for copy in small[3:5]:
        copy.wait()
    weigh(order[0])
    for copy in small[:3]:
        copy.wait()
    pl.semaphore_wait(
        barrier, has_low.astype(jnp.int32) + has_high.astype(jnp.int32) + (mems - 1)
    )
    for way, there in ways:
        @pl.when(there)
        def _(way=way):
            for copy in table_copies(way):
                copy.start()
    token_step(band == 0, band == bands - 1)
    for c in order[1:]:
        weigh(c)
    token_step(band == 1, band == bands - 2)

    def own_dot(t):
        at = pl.ds(pl.multiple_of(t * tile, tile), tile)
        value = slot_dot(source, held, table_s, t, slots, HALO_BLK, 0, own)
        raw[t] = value * (1.0 / target_area[:, at])

    for copy in small[5:]:
        copy.wait()
    sums = lax.dot_general(
        jnp.ones((16, tile), held.dtype),
        held[pl.ds(0, kinds)].reshape(kinds * tile, tile),
        (((1,), (1,)), ((), ())),
        preferred_element_type=jnp.float32,
    )
    for m in range(kinds):
        tile_sum[m:m + 1, :] = sums[0:1, m * tile:(m + 1) * tile]
    for t in range(edge // 2):
        own_dot(t)

    for way, there in ways:
        @pl.when(there)
        def _(way=way):
            for copy in table_copies(1 - way):
                copy.wait_recv()

        @pl.when(jnp.logical_not(there))
        def _(way=way):
            for copy in stand_in(way):
                copy.wait()

    token_step(band == 2, band == bands - 3)

    reaches = (
        (HALO_BLK - own, own - HALO_BLK, own),
        (HALO_BLK + own, 0, HALO_BLK),
    )
    left, right = slot_marks(table_v[...], slots, HALO_BLK, True, own, kinds)
    for way, there in ways:
        a, b = slot_marks(near_v[way], slots, reaches[way][0], there, own, kinds)
        left, right = left + a, right + b
    uses = lax.dot_general(
        jnp.concatenate(left, axis=1),
        jnp.concatenate(right, axis=1),
        (((1,), (1,)), ((), ())),
        preferred_element_type=jnp.float32,
    )
    coef[...] = jnp.dot(
        uses, tile_sum[...], precision=lax.Precision.HIGHEST, preferred_element_type=jnp.float32
    )

    per = own // edge

    def one_edge(j, carry):
        for way, there in ways:
            first = 0 if way == 0 else targets - edge
            value = slot_dot(source, held, near_s.at[way], first + j, slots, *reaches[way])
            made[way, j] = value.astype(made.dtype)
        own_dot(edge // 2 + j)
        total = target_sum[...]
        for i in range(per):
            s = j * per + i
            total = total + source[s].astype(jnp.float32) * coef[pl.ds(s, 1), :]
        target_sum[...] = total
        for way, there in ways:
            @pl.when(there)
            def _(way=way):
                edge_copy(way, j).start()
        return carry

    lax.fori_loop(0, edge, one_edge, 0)

    rows[0:1, :] = row_of(source_sum[...])
    rows[1:2, :] = row_of(target_sum[...])
    rows[2:3, :] = jnp.broadcast_to(
        jnp.sum(target_area[...], axis=1, keepdims=True), (1, columns)
    )
    rows[3:8, :] = jnp.zeros((5, columns), jnp.float32)

    def place(step):
        other = lax.rem(me + step, count)
        return {"mem": other // bands, "band": lax.rem(other, bands)}

    def row_copy(step):
        return pltpu.make_async_remote_copy(
            src_ref=rows,
            dst_ref=landed.at[step],
            send_sem=row_send.at[step],
            recv_sem=row_recv.at[step],
            device_id=place(step),
            device_id_type=MESH,
        )

    def begin(step, carry):
        row_copy(step).start()
        return carry

    def end(step, carry):
        row_copy(step).wait()
        return carry

    token_step(band > 2, band < bands - 3)
    lax.fori_loop(1, count, begin, 0)
    landed[0] = rows[...]

    done = edge // 2 + edge
    for t in range(done, 2 * edge):
        own_dot(t)

    def own_group(g, carry):
        for u in range(edge):
            own_dot(g * edge + u)
        return carry

    lax.fori_loop(2, targets // edge, own_group, 0)

    for way, there in ways:
        @pl.when(there)
        def _(way=way):
            for copy in table_copies(way):
                copy.wait_send()

    lax.fori_loop(1, count, end, 0)
    for m in range(mems):
        total = jnp.zeros(rows.shape, jnp.float32)
        for b in range(bands):
            total = total + landed[lax.rem(me - (m * bands + b) + count, count)]
        totals[m] = total
    mine = totals[mem]
    fix = (mine[0:1, :] - mine[1:2, :]) / mine[2:3, :]
    fix_ref[...] = jnp.broadcast_to(fix, (fix_ref.shape[1], fix.shape[1])).T

    def add(j, carry):
        for way, there in ((0, has_low), (1, has_high)):
            @pl.when(there)
            def _(way=way):
                edge_copy(way, j).wait_recv()
                t = j if way == 0 else targets - edge + j
                at = pl.ds(pl.multiple_of(t * tile, tile), tile)
                share = 1.0 / target_area[:, at]
                raw[t] = raw[t] + came[way, j].astype(jnp.float32) * share
        return carry

    lax.fori_loop(0, edge, add, 0)

    for way, there in ways:
        @pl.when(there)
        def _(way=way):
            def sent(j, carry):
                edge_copy(way, j).wait_send()
                return carry

            lax.fori_loop(0, edge, sent, 0)


def main_call(fields, mask, area, target_area, tiles, tile_t, block_t, live):
    bands, mems = lax.axis_size("band"), lax.axis_size("mem")
    rows, snaps, cells = fields.shape
    columns = rows * snaps
    slots, targets = tile_t.shape
    count, tile = tiles.shape[0], tiles.shape[1]
    own = cells // tile
    edge = HALO_BLK // (own // targets)
    dma = pltpu.SemaphoreType.DMA
    peers = bands * mems
    lines = 2 * slots + 1
    return pl.pallas_call(
        functools.partial(main_kernel, bands, mems, edge),
        in_specs=[HBM] * 8,
        out_specs=(VMEM, VMEM, VMEM),
        out_shape=(
            jax.ShapeDtypeStruct((targets, columns, tile), jnp.float32),
            jax.ShapeDtypeStruct((mems, 8, columns), jnp.float32),
            jax.ShapeDtypeStruct((columns, tile), jnp.float32),
        ),
        scratch_shapes=[
            pltpu.VMEM(mask.shape, mask.dtype),
            pltpu.VMEM(area.shape, area.dtype),
            pltpu.VMEM(target_area.shape, target_area.dtype),
            pltpu.VMEM((lines, targets), jnp.int32),
            pltpu.SMEM((lines, targets), jnp.int32),
            pltpu.VMEM((2, lines, targets), jnp.int32),
            pltpu.SMEM((2, lines, targets), jnp.int32),
            pltpu.VMEM(fields.shape, fields.dtype),
            pltpu.VMEM((own, columns, tile), jnp.bfloat16),
            pltpu.VMEM((count + 1, tile, tile), tiles.dtype),
            pltpu.VMEM((2, edge, columns, tile), SEND_TYPE),
            pltpu.VMEM((2, edge, columns, tile), SEND_TYPE),
            pltpu.VMEM((8, columns), jnp.float32),
            pltpu.VMEM((peers, 8, columns), jnp.float32),
            pltpu.VMEM((columns, tile), jnp.float32),
            pltpu.VMEM((columns, tile), jnp.float32),
            pltpu.VMEM((count, tile), jnp.float32),
            pltpu.VMEM((own, tile), jnp.float32),
            dma((own // HALO_BLK,)),
            dma((10,)),
            dma((2, 6)),
            dma((2, 2)),
            dma((2, 2)),
            dma((2, edge)),
            dma((2, edge)),
            dma((peers,)),
            dma((peers,)),
            pltpu.SemaphoreType.REGULAR((2,)),
        ],
        compiler_params=pltpu.CompilerParams(
            collective_id=0, has_side_effects=True, vmem_limit_bytes=32 << 20
        ),
    )(*[pltpu.with_memory_space_constraint(a, pltpu.HBM) for a in (fields, mask, area, target_area, tiles, tile_t, block_t, live)])


def finish_kernel(fields, snaps, raw_ref, fix_ref, totals_ref, out_ref, mean_ref, ensemble_ref):
    count, columns, tile = raw_ref.shape
    fix = fix_ref[...]
    for n in range(count):
        value = raw_ref[n] + fix
        out_ref[:, :, n * tile:(n + 1) * tile] = value.reshape(columns // snaps, snaps, tile)

    @pl.when(pl.program_id(0) == 1)
    def _():
        mems, members = totals_ref.shape[0], mean_ref.shape[0]
        spot = lax.broadcasted_iota(jnp.int32, (columns, tile), 0)
        lane = lax.broadcasted_iota(jnp.int32, (columns, tile), 1)
        chosen = lax.rem(spot, snaps) == lane
        summed = jnp.zeros((fields, snaps), jnp.float32)

        def table(m):
            row = totals_ref[m, 0:1, :] / totals_ref[m, 2:3, :]
            column = jnp.broadcast_to(row, (tile, columns)).T
            spread = jnp.where(chosen, column, 0.0).reshape(columns // snaps, snaps, tile)
            return jnp.sum(spread, axis=1)[:, 0:snaps]

        mine = table(lax.axis_index("mem"))
        for n in range(members):
            mean_ref[n] = mine[n * fields:(n + 1) * fields]
        for m in range(mems):
            all_of = table(m)
            for n in range(members):
                summed = summed + all_of[n * fields:(n + 1) * fields]
        ensemble_ref[...] = summed / (mems * members)


def finish(raw, fix, totals, members, fields, snaps):
    targets, columns, tile = raw.shape
    steps = 2
    part = targets // steps
    rows = members * fields
    return pl.pallas_call(
        functools.partial(finish_kernel, fields, snaps),
        grid=(steps,),
        in_specs=[
            pl.BlockSpec((part, columns, tile), lambda i: (i, 0, 0)),
            pl.BlockSpec((columns, tile), lambda i: (0, 0)),
            pl.BlockSpec(totals.shape, lambda i: (0, 0, 0)),
        ],
        out_specs=(
            pl.BlockSpec((rows, snaps, part * tile), lambda i: (0, 0, i)),
            pl.BlockSpec((members, fields, snaps), lambda i: (0, 0, 0)),
            pl.BlockSpec((fields, snaps), lambda i: (0, 0)),
        ),
        out_shape=(
            jax.ShapeDtypeStruct((rows, snaps, targets * tile), jnp.float32),
            jax.ShapeDtypeStruct((members, fields, snaps), jnp.float32),
            jax.ShapeDtypeStruct((fields, snaps), jnp.float32),
        ),
        compiler_params=pltpu.CompilerParams(vmem_limit_bytes=16 << 20),
    )(raw, fix, totals)


def on_device(
    surface_fields, land_mask, source_area, target_area, weight_tiles, tile_of, block_of, live_slots
):
    members, fields, snaps, cells = surface_fields.shape
    targets = tile_of.shape[0]
    target_cells = target_area.shape[0]
    raw, totals, fix = main_call(
        surface_fields.reshape(members * fields, snaps, cells),
        land_mask.reshape(1, cells),
        source_area.reshape(1, cells),
        target_area.reshape(1, target_cells),
        weight_tiles,
        tile_of.T,
        block_of.T,
        live_slots.reshape(1, targets),
    )
    regridded, conserved, ensemble = finish(raw, fix, totals, members, fields, snaps)
    return regridded.reshape(members, fields, snaps, target_cells), conserved, ensemble


def solution(mesh):
    placed = (
        P(("grp", "mem"), "fld", None, "band"),
        P("band"),
        P("band"),
        P("band"),
        P(),
        P("band", None),
        P("band", None),
        P("band"),
    )
    return jax.shard_map(
        on_device,
        mesh=mesh,
        in_specs=placed,
        out_specs=(
            P(("grp", "mem"), "fld", None, "band"),
            P(("grp", "mem"), "fld", None),
            P(("grp", "fld"), None),
        ),
        check_vma=False,
    )
```

time: 28.4 us -> 23.6 us (0.83)
  Pallas kernels: 27.6 us -> 22.8 us
    pallas_call x1, Pallas kernels: 26.1 us -> 21.4 us  [main_call(): pl.pallas_call(functools.partial(main_kernel, bands, mems, edge), in_spec...]
where the time goes in v2:
time: 23.6 us; the launch traced here: 23.5 us
  Pallas kernels  22.8 us (97%)
  between operations  0.64 us (3%)
    pallas_call x1, Pallas kernels, main_call(): pl.pallas_call(functools.partial(main_kernel, bands, mems, edge), in_spec...  21.4 us
    pallas_call x1, Pallas kernels, finish(): pl.pallas_call(functools.partial(finish_kernel, fields, snaps), grid=(ste...  1.46 us

profile of v2, /device:TPU:0, one launch (start us, length us, event | category | flops | bytes accessed | tf_op | source)
XLA Modules:
  0.0 23.5 jit_solution(4006584207847889373)
XLA Ops:
  0.6 21.4 %shard_map.103 = (f32[32,128,128]{2,1,0:T(8,128)S(1)}, f32[2,8,128]{2,1,0:T(8,128)S(1)}, f32[128,128]{1,0:T(8,128)S(1)}) custom-call(bf16[16,8,16384]{2,1,0:T(8,128)(2,1)} %bitcast.8, s32[1,16384]{1,0:T(1,128)} %bitcast.9, f32[1,16384]{1,0:T(1,128)} %bitcast.10, f32[1,4096]{1,0:T(1,128)} %bitcast.11, bf16[16,128,128]{2,1,0:T(8,128)(2,1)} %tiles.1, ...), custom_call_target="tpu_custom_call" | custom-call | tf_op jit(solution)/shard_map/pallas_call | solution.py:363
  22.0 1.5 %shard_map.104 = (f32[16,8,4096]{2,1,0:T(8,128)}, f32[4,4,8]{2,1,0:T(4,128)}, f32[4,8]{1,0:T(4,128)}) custom-call(f32[32,128,128]{2,1,0:T(8,128)S(1)} %get-tuple-element.9.raw_ref, f32[128,128]{1,0:T(8,128)S(1)} %get-tuple-element.10.fix_ref, f32[2,8,128]{2,1,0:T(8,128)S(1)} %get-tuple-element.11.totals_ref), custom_call_target="tpu_custom_call" | custom-call | tf_op jit(solution)/shard_map/pallas_call | solution.py:444

commit v3 on v2

--- a/solution.py
+++ b/solution.py
@@ -8,6 +8,8 @@
 from jax.sharding import PartitionSpec as P
 
 HALO_BLK = 32
+RING = 3
+EARLY = 12
 SEND_TYPE = jnp.bfloat16
 MESH = pl.DeviceIdType.MESH
 HBM = pl.BlockSpec(memory_space=pltpu.HBM)
@@ -18,42 +20,72 @@
     return jnp.sum(sums.T, axis=0, keepdims=True)
 
 
-def slot_dot(source, held, table, n, slots, shift, low, high):
-    used, zero_tile = table[2 * slots, n], held.shape[0] - 1
+def slot_pair(source, held, job, p):
+    table, n, slots, shift, low, high = job
+    tile, zero_tile = held.shape[1], held.shape[0] - 1
     left, right = [], []
-    for k in range(slots):
+    for k in (2 * p, 2 * p + 1):
         block = table[slots + k, n] - shift
-        keep = (k < used) & (block >= low) & (block < high)
+        keep = (k < table[2 * slots, n]) & (block >= low) & (block < high)
         left.append(source[jnp.where(keep, block, low)])
         right.append(held[jnp.where(keep, table[k, n], zero_tile)])
-    return jnp.dot(
-        jnp.concatenate(left, axis=1),
-        jnp.concatenate(right, axis=0),
-        preferred_element_type=jnp.float32,
-    )
-
-
-def slot_marks(table, slots, shift, there, own, count):
-    targets = table.shape[1]
-    pieces = slots // 8
-    blank = jnp.full((8, 128 - pieces * targets), -1, jnp.int32)
-    live = (lax.broadcasted_iota(jnp.int32, (slots, targets), 0) < table[2 * slots:2 * slots + 1]) & there
-    blocks = jnp.where(live, table[slots:2 * slots] - shift, -1)
-    kinds = table[0:slots]
-    rows = [jnp.concatenate([a[8 * p:8 * p + 8] for p in range(pieces)] + [blank], axis=1) for a in (blocks, kinds)]
+    right = jnp.concatenate(right, axis=0)
+    return jnp.concatenate(left, axis=1), jnp.concatenate([right, jnp.zeros_like(right)], axis=1)
+
+
+def issue(source, held, jobs, accs):
+    slots = jobs[0][2]
+    for p in range(slots // 2):
+        for unit, job in enumerate(jobs):
+            left, right = slot_pair(source, held, job, p)
+            pltpu.matmul_push_rhs(right, staging_register=p % 2, mxu_index=unit)
+            pltpu.matmul_acc_lhs(accs[unit], left, load_staged_rhs=p % 2)
+
+
+def one_hot(blocks, kinds, own, count):
     spot = lax.broadcasted_iota(jnp.int32, (own, 128), 0)
     kind = lax.broadcasted_iota(jnp.int32, (count, 128), 0)
-    left = [jnp.where(rows[0][r:r + 1] == spot, 1.0, 0.0).astype(jnp.bfloat16) for r in range(8)]
-    right = [jnp.where(rows[1][r:r + 1] == kind, 1.0, 0.0).astype(jnp.bfloat16) for r in range(8)]
+    left, right = [], []
+    for r in range(8):
+        left.append(jnp.where(blocks[r:r + 1] == spot, 1.0, 0.0).astype(jnp.bfloat16))
+        right.append(jnp.where(kinds[r:r + 1] == kind, 1.0, 0.0).astype(jnp.bfloat16))
     return left, right
 
 
-def main_kernel(
-    bands, mems, edge,
+def slot_lanes(parts, slots):
+    found = [[], []]
+    for table, shift, there, first, width in parts:
+        targets = table.shape[1]
+        live = (lax.broadcasted_iota(jnp.int32, (slots, targets), 0) < table[2 * slots:2 * slots + 1]) & there
+        blocks = jnp.where(live, table[slots:2 * slots] - shift, -1)
+        for rows, lanes in ((blocks, found[0]), (table[0:slots], found[1])):
+            lanes += [rows[8 * p:8 * p + 8, first:first + width] for p in range(slots // 8)]
+    used = sum(a.shape[1] for a in found[0])
+    blank = [jnp.full((8, 128 - used), -1, jnp.int32)] if used < 128 else []
+    return [jnp.concatenate(lanes + blank, axis=1) for lanes in found]
+
+
+def main_kernel(bands, mems, edge, *refs):
+    source = refs[19]
+    own, columns, tile = source.shape
+    wide = 2 * tile
+    shapes = [(columns, wide)] * RING + [(own, wide), (2 * 8, wide)]
+
+    def scoped(*accs):
+        half = len(shapes)
+        main_body(bands, mems, edge, accs[:half], accs[half:], *refs)
+
+    pl.run_scoped(
+        scoped, *[pltpu.ACC(unit)(shape, jnp.float32) for unit in (0, 1) for shape in shapes]
+    )
+
+
+def main_body(
+    bands, mems, edge, first_accs, second_accs,
     fields, mask_h, area_h, target_area_h, tiles, tile_h, block_h, live_h,
     raw, totals, fix_ref,
     mask, area, target_area, table_v, table_s, near_v, near_s,
-    stage, source, held, made, came, rows, landed, source_sum, target_sum, tile_sum, coef,
+    stage, source, held, made, came, rows, landed, source_sum, target_sum, tile_sum, uses, coef,
     load_sem, small_sem, near_sem, table_send, table_recv, edge_send, edge_recv, row_send, row_recv, token,
 ):
     band, mem = lax.axis_index("band"), lax.axis_index("mem")
@@ -65,7 +97,6 @@
     has_low, has_high = band > 0, band < bands - 1
     chunk = HALO_BLK * tile
     chunks = own // HALO_BLK
-    order = [0, chunks - 1] + list(range(1, chunks - 1))
     ways = ((0, has_high), (1, has_low))
 
     def neighbour(way):
@@ -101,11 +132,11 @@
     ]
     for copy in small[:5]:
         copy.start()
-    for c in order[:2]:
+    for c in range(2):
         loads[c].start()
     for copy in small[5:]:
         copy.start()
-    for c in order[2:]:
+    for c in range(2, chunks):
         loads[c].start()
 
     def stand_in(way):
@@ -149,20 +180,19 @@
     source_sum[...] = jnp.zeros((columns, tile), jnp.float32)
     target_sum[...] = jnp.zeros((columns, tile), jnp.float32)
 
+    def weigh_block(n):
+        at = pl.ds(n * tile if isinstance(n, int) else pl.multiple_of(n * tile, tile), tile)
+        scale = area[:, at] * mask[:, at].astype(jnp.float32)
+        part = stage[:, :, at].astype(jnp.float32).reshape(columns, tile) * scale
+        source[n] = part.astype(source.dtype)
+
     def weigh(c):
+        def one(n, carry):
+            weigh_block(n)
+            return carry
+
         loads[c].wait()
-
-        def one(n, running):
-            at = pl.ds(pl.multiple_of(n * tile, tile), tile)
-            scale = area[:, at] * mask[:, at].astype(jnp.float32)
-            part = stage[:, :, at].astype(jnp.float32).reshape(columns, tile) * scale
-            part = part.astype(source.dtype)
-            source[n] = part
-            return running + part.astype(jnp.float32)
-
-        source_sum[...] = lax.fori_loop(
-            c * HALO_BLK, (c + 1) * HALO_BLK, one, source_sum[...], unroll=4
-        )
+        lax.fori_loop(c * HALO_BLK, (c + 1) * HALO_BLK, one, 0, unroll=8)
 
     def token_step(up, down):
         for way, at, first in ((0, up, band == 0), (1, down, band == bands - 1)):
@@ -180,7 +210,7 @@
 
     for copy in small[3:5]:
         copy.wait()
-    weigh(order[0])
+    weigh(0)
     for copy in small[:3]:
         copy.wait()
     pl.semaphore_wait(
@@ -192,27 +222,134 @@
             for copy in table_copies(way):
                 copy.start()
     token_step(band == 0, band == bands - 1)
-    for c in order[1:]:
-        weigh(c)
+    weigh(1)
     token_step(band == 1, band == bands - 2)
 
-    def own_dot(t):
-        at = pl.ds(pl.multiple_of(t * tile, tile), tile)
-        value = slot_dot(source, held, table_s, t, slots, HALO_BLK, 0, own)
-        raw[t] = value * (1.0 / target_area[:, at])
+    rings = list(zip(first_accs[:RING], second_accs[:RING]))
+    count_accs = (first_accs[RING], second_accs[RING])
+    small_accs = (first_accs[RING + 1], second_accs[RING + 1])
+
+    def own_pair(t):
+        def sink(values):
+            for u, value in enumerate(values):
+                at = pl.ds(pl.multiple_of((t + u) * tile, tile), tile)
+                raw[t + u] = value * (1.0 / target_area[:, at])
+
+        return [(table_s, t + u, slots, HALO_BLK, 0, own) for u in (0, 1)], sink
+
+    reaches = (
+        (HALO_BLK - own, own - HALO_BLK, own),
+        (HALO_BLK + own, 0, HALO_BLK),
+    )
+    firsts = (0, targets - edge)
+
+    def edge_pair(j):
+        def sink(values):
+            for way, value in enumerate(values):
+                made[way, j] = value.astype(made.dtype)
+
+        return [(near_s.at[way], firsts[way] + j, slots, *reaches[way]) for way in (0, 1)], sink
+
+    def stream(pairs, between=()):
+        ready = None
+        for i, (jobs, sink) in enumerate(pairs):
+            issue(source, held, jobs, rings[i % RING])
+            if ready is not None:
+                ready[1]([pltpu.matmul_pop(acc)[:, :tile] for acc in ready[0]])
+            ready = (rings[i % RING], sink)
+            if i < len(between):
+                between[i]()
+        ready[1]([pltpu.matmul_pop(acc)[:, :tile] for acc in ready[0]])
+
+    def tile_sums():
+        lane = lax.broadcasted_iota(jnp.int32, (16, 2 * tile), 1)
+        line = lax.broadcasted_iota(jnp.int32, (16, 2 * tile), 0)
+        ones = jnp.where(lane // tile == line, 1.0, 0.0).astype(held.dtype)
+        for g in range(kinds // 4):
+            unit = g % 2
+            four = [held[4 * g + i] for i in range(4)]
+            right = jnp.concatenate(
+                [jnp.concatenate(four[:2], axis=1), jnp.concatenate(four[2:], axis=1)], axis=0
+            )
+            pltpu.matmul_push_rhs(right, staging_register=0, mxu_index=unit, transpose=True)
+            pltpu.matmul_acc_lhs(small_accs[unit], ones, load_staged_rhs=0)
+            sums = pltpu.matmul_pop(small_accs[unit])
+            for i in range(4):
+                half = i // 2
+                tile_sum[4 * g + i:4 * g + i + 1, :] = sums[i % 2:i % 2 + 1, half * tile:(half + 1) * tile]
+
+    def count_uses(parts):
+        left, right = one_hot(*slot_lanes(parts, slots), own, kinds)
+        blank = jnp.zeros((2 * tile - 6 * kinds, 2 * tile), held.dtype)
+        for r in range(0, 8, 2):
+            unit = (r // 2) % 2
+            marks = jnp.concatenate(right[r:r + 2], axis=1)
+            pltpu.matmul_push_rhs(
+                jnp.concatenate([marks] * 6 + [blank], axis=0),
+                staging_register=0, mxu_index=unit, transpose=True,
+            )
+            pltpu.matmul_acc_lhs(
+                count_accs[unit], jnp.concatenate(left[r:r + 2], axis=1), load_staged_rhs=0
+            )
+
+    def use_counts(add):
+        found = (pltpu.matmul_pop(count_accs[0]) + pltpu.matmul_pop(count_accs[1]))[:, :tile]
+        found = found + uses[...] if add else found
+        uses[...] = found
+        high = jnp.floor(found * (1.0 / 256.0)) * 256.0
+        lane = lax.broadcasted_iota(jnp.int32, found.shape, 1)
+        left = jnp.where(lane < 3 * kinds, found - high, high).astype(held.dtype)
+        rest, pieces = tile_sum[...], []
+        for _ in range(3):
+            pieces.append(rest.astype(held.dtype))
+            rest = rest - pieces[-1].astype(jnp.float32)
+        right = jnp.concatenate(
+            pieces * 2 + [jnp.zeros((2 * tile - 6 * kinds, tile), held.dtype)], axis=0
+        )
+        pltpu.matmul_push_rhs(
+            jnp.concatenate([right, jnp.zeros_like(right)], axis=1), staging_register=0, mxu_index=0
+        )
+        pltpu.matmul_acc_lhs(
+            count_accs[0], jnp.concatenate([left, jnp.zeros_like(left)], axis=1), load_staged_rhs=0
+        )
+
+    def keep_coef():
+        coef[...] = pltpu.matmul_pop(count_accs[0])[:, :tile]
+
+    def sum_blocks(first, number):
+        plain, scaled = source_sum[...], target_sum[...]
+        for n in range(first, first + number):
+            part = source[n].astype(jnp.float32)
+            plain = plain + part
+            scaled = scaled + part * coef[n:n + 1, :]
+        source_sum[...] = plain
+        target_sum[...] = scaled
 
     for copy in small[5:]:
         copy.wait()
-    sums = lax.dot_general(
-        jnp.ones((16, tile), held.dtype),
-        held[pl.ds(0, kinds)].reshape(kinds * tile, tile),
-        (((1,), (1,)), ((), ())),
-        preferred_element_type=jnp.float32,
-    )
-    for m in range(kinds):
-        tile_sum[m:m + 1, :] = sums[0:1, m * tile:(m + 1) * tile]
-    for t in range(edge // 2):
-        own_dot(t)
+    for c in range(2, chunks):
+        loads[c].wait()
+    tile_sums()
+    count_uses([(table_v[...], HALO_BLK, True, 0, targets)])
+    early = EARLY
+    lots = early // 2
+    fresh = list(range(2 * HALO_BLK, own))
+    share = -(-len(fresh) // (lots - 1))
+
+    def beside(i):
+        for n in fresh[i * share:(i + 1) * share]:
+            weigh_block(n)
+        if i == 0:
+            use_counts(False)
+        if i == 1:
+            keep_coef()
+        if i == lots - 1:
+            sum_blocks(HALO_BLK, own - 2 * HALO_BLK)
+
+    stream(
+        [own_pair(t) for t in range(0, early, 2)],
+        [functools.partial(beside, i) for i in range(lots)],
+    )
 
     for way, there in ways:
         @pl.when(there)
@@ -227,44 +364,34 @@
 
     token_step(band == 2, band == bands - 3)
 
-    reaches = (
-        (HALO_BLK - own, own - HALO_BLK, own),
-        (HALO_BLK + own, 0, HALO_BLK),
-    )
-    left, right = slot_marks(table_v[...], slots, HALO_BLK, True, own, kinds)
-    for way, there in ways:
-        a, b = slot_marks(near_v[way], slots, reaches[way][0], there, own, kinds)
-        left, right = left + a, right + b
-    uses = lax.dot_general(
-        jnp.concatenate(left, axis=1),
-        jnp.concatenate(right, axis=1),
-        (((1,), (1,)), ((), ())),
-        preferred_element_type=jnp.float32,
-    )
-    coef[...] = jnp.dot(
-        uses, tile_sum[...], precision=lax.Precision.HIGHEST, preferred_element_type=jnp.float32
-    )
-
-    per = own // edge
-
-    def one_edge(j, carry):
-        for way, there in ways:
-            first = 0 if way == 0 else targets - edge
-            value = slot_dot(source, held, near_s.at[way], first + j, slots, *reaches[way])
-            made[way, j] = value.astype(made.dtype)
-        own_dot(edge // 2 + j)
-        total = target_sum[...]
-        for i in range(per):
-            s = j * per + i
-            total = total + source[s].astype(jnp.float32) * coef[pl.ds(s, 1), :]
-        target_sum[...] = total
+    def send_edge(j):
         for way, there in ways:
             @pl.when(there)
             def _(way=way):
                 edge_copy(way, j).start()
-        return carry
-
-    lax.fori_loop(0, edge, one_edge, 0)
+
+    stream([edge_pair(0)])
+    send_edge(0)
+
+    near = [(near_v[way], reaches[way][0], there, firsts[way], edge) for way, there in ways]
+
+    def last_sums():
+        keep_coef()
+        sum_blocks(0, HALO_BLK)
+
+    done = early
+    stream(
+        [edge_pair(1), edge_pair(2), own_pair(done), own_pair(done + 2)],
+        (
+            lambda: count_uses(near),
+            lambda: use_counts(True),
+            last_sums,
+            lambda: sum_blocks(own - HALO_BLK, HALO_BLK),
+        ),
+    )
+    send_edge(1)
+    send_edge(2)
+    done += 4
 
     rows[0:1, :] = row_of(source_sum[...])
     rows[1:2, :] = row_of(target_sum[...])
@@ -299,16 +426,22 @@
     lax.fori_loop(1, count, begin, 0)
     landed[0] = rows[...]
 
-    done = edge // 2 + edge
-    for t in range(done, 2 * edge):
-        own_dot(t)
-
-    def own_group(g, carry):
-        for u in range(edge):
-            own_dot(g * edge + u)
+    steps = (edge - 4) // 2
+
+    def two_edges(i, carry):
+        j, t = 3 + 2 * i, done + 2 * i
+        stream([edge_pair(j), edge_pair(j + 1), own_pair(t)])
+        send_edge(j)
+        send_edge(j + 1)
         return carry
 
-    lax.fori_loop(2, targets // edge, own_group, 0)
+    lax.fori_loop(0, steps, two_edges, 0)
+    last = done + 2 * steps
+    stream([edge_pair(j) for j in range(3 + 2 * steps, edge)] + [own_pair(last)])
+    for j in range(3 + 2 * steps, edge):
+        send_edge(j)
+    last += 2
+    stream([own_pair(t) for t in range(last, targets, 2)])
 
     for way, there in ways:
         @pl.when(there)
@@ -388,6 +521,7 @@
             pltpu.VMEM((columns, tile), jnp.float32),
             pltpu.VMEM((count, tile), jnp.float32),
             pltpu.VMEM((own, tile), jnp.float32),
+            pltpu.VMEM((own, tile), jnp.float32),
             dma((own // HALO_BLK,)),
             dma((10,)),
             dma((2, 6)),

time: 23.6 us -> 22 us (0.932)
  Pallas kernels: 22.8 us -> 21.2 us
    pallas_call x1, Pallas kernels: 21.4 us -> 19.8 us  [main_call(): pl.pallas_call(functools.partial(main_kernel, bands, mems, edge), in_spec...]
where the time goes in v3:
time: 22 us; the launch traced here: 21.9 us
  Pallas kernels  21.2 us (96%)
  between operations  0.64 us (3%)
    pallas_call x1, Pallas kernels, main_call(): pl.pallas_call(functools.partial(main_kernel, bands, mems, edge), in_spec...  19.8 us
    pallas_call x1, Pallas kernels, finish(): pl.pallas_call(functools.partial(finish_kernel, fields, snaps), grid=(ste...  1.46 us

profile of v3, /device:TPU:0, one launch (start us, length us, event | category | flops | bytes accessed | tf_op | source)
XLA Modules:
  0.0 21.9 jit_solution(13054110995336106123)
XLA Ops:
  0.6 19.8 %shard_map.103 = (f32[32,128,128]{2,1,0:T(8,128)S(1)}, f32[2,8,128]{2,1,0:T(8,128)S(1)}, f32[128,128]{1,0:T(8,128)S(1)}) custom-call(bf16[16,8,16384]{2,1,0:T(8,128)(2,1)} %bitcast.8, s32[1,16384]{1,0:T(1,128)} %bitcast.9, f32[1,16384]{1,0:T(1,128)} %bitcast.10, f32[1,4096]{1,0:T(1,128)} %bitcast.11, bf16[16,128,128]{2,1,0:T(8,128)(2,1)} %refs_4_.1, ...), custom_call_target="tpu_custom_call" | custom-call | tf_op jit(solution)/shard_map/pallas_call | solution.py:496
  20.4 1.5 %shard_map.104 = (f32[16,8,4096]{2,1,0:T(8,128)}, f32[4,4,8]{2,1,0:T(4,128)}, f32[4,8]{1,0:T(4,128)}) custom-call(f32[32,128,128]{2,1,0:T(8,128)S(1)} %get-tuple-element.9.raw_ref, f32[128,128]{1,0:T(8,128)S(1)} %get-tuple-element.10.fix_ref, f32[2,8,128]{2,1,0:T(8,128)S(1)} %get-tuple-element.11.totals_ref), custom_call_target="tpu_custom_call" | custom-call | tf_op jit(solution)/shard_map/pallas_call | solution.py:578

commit v4 on v3

--- a/solution.py
+++ b/solution.py
@@ -9,7 +9,7 @@
 
 HALO_BLK = 32
 RING = 3
-EARLY = 12
+EARLY = 8
 SEND_TYPE = jnp.bfloat16
 MESH = pl.DeviceIdType.MESH
 HBM = pl.BlockSpec(memory_space=pltpu.HBM)
@@ -125,16 +125,16 @@
         pltpu.make_async_copy(a, b, small_sem.at[i])
         for i, (a, b) in enumerate(
             [(a, table_v.at[at]) for a, at in lists]
-            + [(mask_h, mask), (area_h, area)]
+            + [(tiles, held.at[pl.ds(0, kinds)]), (mask_h, mask), (area_h, area)]
             + [(a, table_s.at[at]) for a, at in lists]
-            + [(tiles, held.at[pl.ds(0, kinds)]), (target_area_h, target_area)]
+            + [(target_area_h, target_area)]
         )
     ]
-    for copy in small[:5]:
+    for copy in small[:6]:
         copy.start()
     for c in range(2):
         loads[c].start()
-    for copy in small[5:]:
+    for copy in small[6:]:
         copy.start()
     for c in range(2, chunks):
         loads[c].start()
@@ -208,23 +208,6 @@
                     token.at[way], inc=1, device_id=neighbour(way), device_id_type=MESH
                 )
 
-    for copy in small[3:5]:
-        copy.wait()
-    weigh(0)
-    for copy in small[:3]:
-        copy.wait()
-    pl.semaphore_wait(
-        barrier, has_low.astype(jnp.int32) + has_high.astype(jnp.int32) + (mems - 1)
-    )
-    for way, there in ways:
-        @pl.when(there)
-        def _(way=way):
-            for copy in table_copies(way):
-                copy.start()
-    token_step(band == 0, band == bands - 1)
-    weigh(1)
-    token_step(band == 1, band == bands - 2)
-
     rings = list(zip(first_accs[:RING], second_accs[:RING]))
     count_accs = (first_accs[RING], second_accs[RING])
     small_accs = (first_accs[RING + 1], second_accs[RING + 1])
@@ -250,16 +233,19 @@
 
         return [(near_s.at[way], firsts[way] + j, slots, *reaches[way]) for way in (0, 1)], sink
 
-    def stream(pairs, between=()):
-        ready = None
-        for i, (jobs, sink) in enumerate(pairs):
-            issue(source, held, jobs, rings[i % RING])
-            if ready is not None:
-                ready[1]([pltpu.matmul_pop(acc)[:, :tile] for acc in ready[0]])
-            ready = (rings[i % RING], sink)
-            if i < len(between):
-                between[i]()
-        ready[1]([pltpu.matmul_pop(acc)[:, :tile] for acc in ready[0]])
+    state = {"ready": None, "number": 0}
+
+    def read_out():
+        accs, sink = state["ready"]
+        sink([pltpu.matmul_pop(acc)[:, :tile] for acc in accs])
+
+    def put(pair):
+        jobs, sink = pair
+        accs = rings[state["number"] % RING]
+        issue(source, held, jobs, accs)
+        if state["ready"] is not None:
+            read_out()
+        state["ready"], state["number"] = (accs, sink), state["number"] + 1
 
     def tile_sums():
         lane = lax.broadcasted_iota(jnp.int32, (16, 2 * tile), 1)
@@ -325,31 +311,41 @@
         source_sum[...] = plain
         target_sum[...] = scaled
 
-    for copy in small[5:]:
+    def enter():
+        pl.semaphore_wait(
+            barrier, has_low.astype(jnp.int32) + has_high.astype(jnp.int32) + (mems - 1)
+        )
+        for way, there in ways:
+            @pl.when(there)
+            def _(way=way):
+                for copy in table_copies(way):
+                    copy.start()
+        token_step(band == 0, band == bands - 1)
+
+    for copy in small[:3]:
         copy.wait()
-    for c in range(2, chunks):
-        loads[c].wait()
+
+    enter()
+
+    small[3].wait()
     tile_sums()
     count_uses([(table_v[...], HALO_BLK, True, 0, targets)])
+    use_counts(False)
+    keep_coef()
+    for copy in small[4:6]:
+        copy.wait()
+    weigh(0)
+    for c in range(1, chunks):
+        weigh(c)
+    token_step(band == 1, band == bands - 2)
+
+    for copy in small[6:]:
+        copy.wait()
     early = EARLY
-    lots = early // 2
-    fresh = list(range(2 * HALO_BLK, own))
-    share = -(-len(fresh) // (lots - 1))
-
-    def beside(i):
-        for n in fresh[i * share:(i + 1) * share]:
-            weigh_block(n)
-        if i == 0:
-            use_counts(False)
-        if i == 1:
-            keep_coef()
-        if i == lots - 1:
+    for t in range(0, early, 2):
+        put(own_pair(t))
+        if t == 0:
             sum_blocks(HALO_BLK, own - 2 * HALO_BLK)
-
-    stream(
-        [own_pair(t) for t in range(0, early, 2)],
-        [functools.partial(beside, i) for i in range(lots)],
-    )
 
     for way, there in ways:
         @pl.when(there)
@@ -362,6 +358,7 @@
             for copy in stand_in(way):
                 copy.wait()
 
+
     token_step(band == 2, band == bands - 3)
 
     def send_edge(j):
@@ -370,29 +367,20 @@
             def _(way=way):
                 edge_copy(way, j).start()
 
-    stream([edge_pair(0)])
+    near = [(near_v[way], reaches[way][0], there, firsts[way], edge) for way, there in ways]
+    put(edge_pair(0))
+    count_uses(near)
+    put(edge_pair(1))
+    use_counts(True)
     send_edge(0)
-
-    near = [(near_v[way], reaches[way][0], there, firsts[way], edge) for way, there in ways]
-
-    def last_sums():
-        keep_coef()
-        sum_blocks(0, HALO_BLK)
-
-    done = early
-    stream(
-        [edge_pair(1), edge_pair(2), own_pair(done), own_pair(done + 2)],
-        (
-            lambda: count_uses(near),
-            lambda: use_counts(True),
-            last_sums,
-            lambda: sum_blocks(own - HALO_BLK, HALO_BLK),
-        ),
-    )
+    put(edge_pair(2))
+    keep_coef()
+    sum_blocks(0, HALO_BLK)
     send_edge(1)
+    put(own_pair(early))
+    sum_blocks(own - HALO_BLK, HALO_BLK)
     send_edge(2)
-    done += 4
-
+    put(edge_pair(3))
     rows[0:1, :] = row_of(source_sum[...])
     rows[1:2, :] = row_of(target_sum[...])
     rows[2:3, :] = jnp.broadcast_to(
@@ -426,22 +414,14 @@
     lax.fori_loop(1, count, begin, 0)
     landed[0] = rows[...]
 
-    steps = (edge - 4) // 2
-
-    def two_edges(i, carry):
-        j, t = 3 + 2 * i, done + 2 * i
-        stream([edge_pair(j), edge_pair(j + 1), own_pair(t)])
-        send_edge(j)
-        send_edge(j + 1)
-        return carry
-
-    lax.fori_loop(0, steps, two_edges, 0)
-    last = done + 2 * steps
-    stream([edge_pair(j) for j in range(3 + 2 * steps, edge)] + [own_pair(last)])
-    for j in range(3 + 2 * steps, edge):
-        send_edge(j)
-    last += 2
-    stream([own_pair(t) for t in range(last, targets, 2)])
+    for j in range(4, edge):
+        put(edge_pair(j))
+        send_edge(j - 1)
+    for t in range(early + 2, targets, 2):
+        put(own_pair(t))
+        if t == early + 2:
+            send_edge(edge - 1)
+    read_out()
 
     for way, there in ways:
         @pl.when(there)

time: 22 us -> 19.9 us (0.905)
  Pallas kernels: 21.2 us -> 19 us
    pallas_call x1, Pallas kernels: 19.8 us -> 17.6 us  [main_call(): pl.pallas_call(functools.partial(main_kernel, bands, mems, edge), in_spec...]
where the time goes in v4:
time: 19.9 us; the launch traced here: 19.7 us
  Pallas kernels  19 us (95%)
  between operations  0.64 us (3%)
    pallas_call x1, Pallas kernels, main_call(): pl.pallas_call(functools.partial(main_kernel, bands, mems, edge), in_spec...  17.6 us
    pallas_call x1, Pallas kernels, finish(): pl.pallas_call(functools.partial(finish_kernel, fields, snaps), grid=(ste...  1.46 us

profile of v4, /device:TPU:0, one launch (start us, length us, event | category | flops | bytes accessed | tf_op | source)
XLA Modules:
  0.0 19.7 jit_solution(12405209402179471947)
XLA Ops:
  0.6 17.6 %shard_map.103 = (f32[32,128,128]{2,1,0:T(8,128)S(1)}, f32[2,8,128]{2,1,0:T(8,128)S(1)}, f32[128,128]{1,0:T(8,128)S(1)}) custom-call(bf16[16,8,16384]{2,1,0:T(8,128)(2,1)} %bitcast.8, s32[1,16384]{1,0:T(1,128)} %bitcast.9, f32[1,16384]{1,0:T(1,128)} %bitcast.10, f32[1,4096]{1,0:T(1,128)} %bitcast.11, bf16[16,128,128]{2,1,0:T(8,128)(2,1)} %refs_4_.1, ...), custom_call_target="tpu_custom_call" | custom-call | tf_op jit(solution)/shard_map/pallas_call | solution.py:476
  18.2 1.5 %shard_map.104 = (f32[16,8,4096]{2,1,0:T(8,128)}, f32[4,4,8]{2,1,0:T(4,128)}, f32[4,8]{1,0:T(4,128)}) custom-call(f32[32,128,128]{2,1,0:T(8,128)S(1)} %get-tuple-element.9.raw_ref, f32[128,128]{1,0:T(8,128)S(1)} %get-tuple-element.10.fix_ref, f32[2,8,128]{2,1,0:T(8,128)S(1)} %get-tuple-element.11.totals_ref), custom_call_target="tpu_custom_call" | custom-call | tf_op jit(solution)/shard_map/pallas_call | solution.py:558

commit v5 on v4

--- a/solution.py
+++ b/solution.py
@@ -192,7 +192,7 @@
             return carry
 
         loads[c].wait()
-        lax.fori_loop(c * HALO_BLK, (c + 1) * HALO_BLK, one, 0, unroll=8)
+        lax.fori_loop(c * HALO_BLK, (c + 1) * HALO_BLK, one, 0, unroll=HALO_BLK)
 
     def token_step(up, down):
         for way, at, first in ((0, up, band == 0), (1, down, band == bands - 1)):
@@ -439,18 +439,20 @@
     fix = (mine[0:1, :] - mine[1:2, :]) / mine[2:3, :]
     fix_ref[...] = jnp.broadcast_to(fix, (fix_ref.shape[1], fix.shape[1])).T
 
-    def add(j, carry):
-        for way, there in ((0, has_low), (1, has_high)):
-            @pl.when(there)
-            def _(way=way):
-                edge_copy(way, j).wait_recv()
-                t = j if way == 0 else targets - edge + j
-                at = pl.ds(pl.multiple_of(t * tile, tile), tile)
-                share = 1.0 / target_area[:, at]
-                raw[t] = raw[t] + came[way, j].astype(jnp.float32) * share
-        return carry
-
-    lax.fori_loop(0, edge, add, 0)
+    for way, there in ((0, has_low), (1, has_high)):
+        @pl.when(there)
+        def _(way=way):
+            def add(g, carry):
+                for j in (2 * g, 2 * g + 1):
+                    edge_copy(way, j).wait_recv()
+                for j in (2 * g, 2 * g + 1):
+                    t = j if way == 0 else targets - edge + j
+                    at = pl.ds(pl.multiple_of(t * tile, tile), tile)
+                    share = 1.0 / target_area[:, at]
+                    raw[t] = raw[t] + came[way, j].astype(jnp.float32) * share
+                return carry
+
+            lax.fori_loop(0, edge // 2, add, 0)
 
     for way, there in ways:
         @pl.when(there)

time: 19.9 us -> 19.6 us (0.985)
  Pallas kernels: 19 us -> 18.8 us
    pallas_call x1, Pallas kernels: 17.6 us -> 17.3 us  [main_call(): pl.pallas_call(functools.partial(main_kernel, bands, mems, edge), in_spec...]
where the time goes in v5:
time: 19.6 us; the launch traced here: 19.4 us
  Pallas kernels  18.8 us (96%)
  between operations  0.64 us (3%)
    pallas_call x1, Pallas kernels, main_call(): pl.pallas_call(functools.partial(main_kernel, bands, mems, edge), in_spec...  17.3 us
    pallas_call x1, Pallas kernels, finish(): pl.pallas_call(functools.partial(finish_kernel, fields, snaps), grid=(ste...  1.46 us

profile of v5, /device:TPU:0, one launch (start us, length us, event | category | flops | bytes accessed | tf_op | source)
XLA Modules:
  0.0 19.4 jit_solution(17748652618363905631)
XLA Ops:
  0.6 17.3 %shard_map.103 = (f32[32,128,128]{2,1,0:T(8,128)S(1)}, f32[2,8,128]{2,1,0:T(8,128)S(1)}, f32[128,128]{1,0:T(8,128)S(1)}) custom-call(bf16[16,8,16384]{2,1,0:T(8,128)(2,1)} %bitcast.8, s32[1,16384]{1,0:T(1,128)} %bitcast.9, f32[1,16384]{1,0:T(1,128)} %bitcast.10, f32[1,4096]{1,0:T(1,128)} %bitcast.11, bf16[16,128,128]{2,1,0:T(8,128)(2,1)} %refs_4_.1, ...), custom_call_target="tpu_custom_call" | custom-call | tf_op jit(solution)/shard_map/pallas_call | solution.py:478
  17.9 1.5 %shard_map.104 = (f32[16,8,4096]{2,1,0:T(8,128)}, f32[4,4,8]{2,1,0:T(4,128)}, f32[4,8]{1,0:T(4,128)}) custom-call(f32[32,128,128]{2,1,0:T(8,128)S(1)} %get-tuple-element.9.raw_ref, f32[128,128]{1,0:T(8,128)S(1)} %get-tuple-element.10.fix_ref, f32[2,8,128]{2,1,0:T(8,128)S(1)} %get-tuple-element.11.totals_ref), custom_call_target="tpu_custom_call" | custom-call | tf_op jit(solution)/shard_map/pallas_call | solution.py:560
